TPU v7x, 256 devices: a 8x8x2 block of a 8x8x16 slice. The times are simulated.
256 devices in a mesh: parts: 2 (over z), seq: 128 (over x, y, core).
Axes of the slice: x: 8, y: 8, z: 2, core: 2. Of those that a mesh axis runs over, the one named last changes fastest.
The devices are a block of a 8x8x16 slice.
Arguments:
- token_ids: int32 [4, 4], P(None, 'parts'), parts along dimension 1, may hold values from 0 to 76031
- lengths: int32 [4], P('parts'), parts along dimension 0, may hold values from 24576 to 32768, as said below
- embed_table: bfloat16 [76032, 5120], P('seq'), may hold values from -6 to 6
- attn_gain: bfloat16 [5120], replicated, may hold values from 0.25 to 1.75
- w_qkv: bfloat16 [5120, 7168], P('seq'), may hold values from -0.3125 to 0.3125
- qkv_bias: float32 [7168], replicated, may hold values from -8 to 8
- cache_keys: bfloat16 [4, 32768, 1024], P('parts', 'seq'), parts along dimension 0, may hold values from -300 to 300
- cache_values: bfloat16 [4, 32768, 1024], P('parts', 'seq'), parts along dimension 0, may hold values from -6 to 6
- w_out: bfloat16 [5120, 5120], P(None, 'seq'), may hold values from -0.078125 to 0.078125
- mlp_gain: bfloat16 [5120], replicated, may hold values from 0.25 to 1.75
- w_gate: bfloat16 [5120, 16384], P(None, 'seq'), may hold values from -0.078125 to 0.078125
- w_up: bfloat16 [5120, 16384], P(None, 'seq'), may hold values from -0.078125 to 0.078125
- w_down: bfloat16 [16384, 5120], P('seq'), may hold values from -0.1875 to 0.1875
Outputs:
- attended: bfloat16 [4, 4, 5120], P(None, 'parts'), parts along dimension 1
- layer_out: bfloat16 [4, 4, 5120], P(None, 'parts', 'seq'), parts along dimension 1
There are 2 independent parts, one for each index of `parts`. A program takes and returns all parts, laid end to end along the dimension named above; an argument that names none is the same for every part. Nothing has to cross between parts.
Inputs may be any that keep to these rules, and one draw needn't show every extreme that they name: Cache positions lengths[b] and later are unused; the first prompt fills the whole cache of 32768 positions.
All inputs are finite; a program needn't handle non-finite values.
Results may differ from a plain program's by a relative error of at most 0.017.
The roundings to bfloat16 on the way count: a program that leaves them out, or rounds other values in their place, can miss the bound.
Values may be sent and summed in bfloat16 or wider, within the bound.
No kernel may reach another device: no remote copies, remote signals or barrier semaphores. Data moves between devices by JAX's collectives and lax.ppermute only.
A program may use at most 128 MiB of HBM per device.

v0:
```python
import math
import jax
import jax.numpy as jnp
from jax import lax
from jax.sharding import Mesh
from jax.sharding import PartitionSpec as P

HEADS = 40
KV_HEADS = 8
HEAD_DIM = 128
SEQ = ("seq_0", "seq_1", "seq_2")
NORM_EPS = 1e-06
ROPE_BASE = 1000000.0
MASKED = -1e30


def gathered_once(array, axis):
    leaves = jax.tree.leaves(array)
    order = sorted(range(len(leaves)), key=lambda k: -leaves[k].size)
    width = (1, *leaves[order[0]].shape)[-1]
    lines = [
        jnp.pad(leaves[k].reshape(-1), (0, -leaves[k].size % width)).reshape(-1, width)
        for k in order
    ]
    both, at, found = (lax.all_gather(jnp.concatenate(lines), axis), 0, {})
    for k, line in zip(order, lines):
        slab = both[:, at : at + len(line)].reshape(len(both), -1)
        found[k] = slab[:, : leaves[k].size].reshape(-1, *leaves[k].shape)
        at += len(line)
    numbers = iter(range(len(leaves)))
    return jax.tree.map(lambda _: found[next(numbers)], array)


def combined_by_axis(array, axes, combine):
    for axis in axes:
        pieces = gathered_once(array, axis)
        array = jax.tree.map(lambda part: part[0], pieces)
        for k in range(1, lax.axis_size(axis)):
            array = combine(array, jax.tree.map(lambda part: part[k], pieces))
    return array


def sum_in_order(parts, axes, order):
    dims = [lax.axis_size(a) for a in axes]
    parts = parts.reshape(*dims, *parts.shape[1:])
    parts = parts.transpose(*order, *range(len(axes), parts.ndim))
    parts = parts.reshape(-1, *parts.shape[len(axes) :])
    for k in order:
        parts = lax.psum_scatter(parts, axes[k], scatter_dimension=0, tiled=True)
    return parts[0]


def cut_along(array, dim, devices):
    before, after = (array.shape[:dim], array.shape[dim + 1 :])
    return jnp.moveaxis(array.reshape(*before, devices, -1, *after), dim, 0)


def scatter_axes(array, axes, order, dim):
    devices = lax.axis_size(axes)
    return sum_in_order(cut_along(array, dim, devices), axes, order)


def rms_normalize(rows, gain):
    mean_square = jnp.mean(rows * rows, axis=-1, keepdims=True)
    return (rows * lax.rsqrt(mean_square + NORM_EPS) * gain.astype(jnp.float32)).astype(
        jnp.bfloat16
    )


def rotate(vectors, positions):
    half_dim = vectors.shape[-1] // 2
    frequency = ROPE_BASE ** (-2.0 * jnp.arange(half_dim, dtype=jnp.float32) / vectors.shape[-1])
    angles = positions.astype(jnp.float32)[..., None, None] * frequency
    cosine = jnp.cos(angles)
    sine_part = jnp.sin(angles)
    widened = vectors.astype(jnp.float32)
    first_half = widened[..., :half_dim]
    second = widened[..., half_dim:]
    joined = jnp.concatenate(
        [first_half * cosine - second * sine_part, second * cosine + first_half * sine_part],
        axis=-1,
    )
    return joined.astype(jnp.bfloat16)


def combine_partials(earlier, latter):
    top_one, total_one, sum_one = earlier
    top_two, total_two, sum_two = latter
    joined_top = jnp.maximum(top_one, top_two)
    scale_one = jnp.exp(top_one - joined_top)
    scale_two = jnp.exp(top_two - joined_top)
    return (
        joined_top,
        total_one * scale_one + total_two * scale_two,
        sum_one * scale_one[..., None] + sum_two * scale_two[..., None],
    )


def body(
    token_ids,
    lengths,
    embed_table,
    attn_gain,
    w_qkv,
    qkv_bias,
    cache_keys,
    cache_values,
    w_out,
    mlp_gain,
    w_gate,
    w_up,
    w_down,
):
    rank = lax.axis_index(SEQ)
    step_count, batch_count = token_ids.shape
    model_width = embed_table.shape[1]
    vocab_rows = embed_table.shape[0]
    query_width = HEADS * HEAD_DIM
    key_width = KV_HEADS * HEAD_DIM
    group_size = HEADS // KV_HEADS
    local_ids = token_ids - rank * vocab_rows
    inside = (local_ids >= 0) & (local_ids < vocab_rows)
    picked = jnp.take(embed_table, jnp.clip(local_ids, 0, vocab_rows - 1), axis=0)
    partial_rows = jnp.where(inside[..., None], picked.astype(jnp.float32), 0.0)
    stream = lax.psum(partial_rows, SEQ)
    normed = rms_normalize(stream, attn_gain).reshape(-1, model_width)
    feature_rows = w_qkv.shape[0]
    normed_local = lax.dynamic_slice_in_dim(normed, rank * feature_rows, feature_rows, 1)
    joint_partial = jnp.dot(normed_local, w_qkv, preferred_element_type=jnp.float32)
    joint_summed = lax.psum(joint_partial, SEQ)
    joint = (joint_summed + qkv_bias).astype(jnp.bfloat16).reshape(step_count, batch_count, -1)
    query_part = joint[..., :query_width].reshape(step_count, batch_count, HEADS, HEAD_DIM)
    key_part = joint[..., query_width : query_width + key_width].reshape(
        step_count, batch_count, KV_HEADS, HEAD_DIM
    )
    value_part = joint[..., query_width + key_width :].reshape(
        step_count, batch_count, KV_HEADS, HEAD_DIM
    )
    positions = lengths[None, :] + jnp.arange(step_count, dtype=jnp.int32)[:, None]
    queries = rotate(query_part, positions)
    new_keys = rotate(key_part, positions)
    grouped = queries.reshape(step_count, batch_count, KV_HEADS, group_size, HEAD_DIM)
    score_scale = 1.0 / math.sqrt(HEAD_DIM)
    local_len = cache_keys.shape[1]
    key_blocks = cache_keys.reshape(batch_count, local_len, KV_HEADS, HEAD_DIM)
    value_blocks = cache_values.reshape(batch_count, local_len, KV_HEADS, HEAD_DIM)
    scores = (
        jnp.einsum("sbkgd,bpkd->bkgsp", grouped, key_blocks, preferred_element_type=jnp.float32)
        * score_scale
    )
    places = rank * local_len + jnp.arange(local_len, dtype=jnp.int32)
    valid = (places[None, :] < lengths[:, None])[:, None, None, None, :]
    masked = jnp.where(valid, scores, MASKED)
    local_top = jnp.max(masked, axis=-1)
    weights = jnp.where(valid, jnp.exp(masked - local_top[..., None]), 0.0)
    local_total = jnp.sum(weights, axis=-1)
    local_sum = jnp.einsum(
        "bkgsp,bpkd->bkgsd",
        weights.astype(jnp.bfloat16),
        value_blocks,
        preferred_element_type=jnp.float32,
    )
    merged_top, merged_total, merged_sum = combined_by_axis(
        (local_top, local_total, local_sum), SEQ, combine_partials
    )
    new_scores = (
        jnp.einsum("sbkgd,tbkd->bkgst", grouped, new_keys, preferred_element_type=jnp.float32)
        * score_scale
    )
    step_index = jnp.arange(step_count, dtype=jnp.int32)
    causal = step_index[:, None] >= step_index[None, :]
    new_masked = jnp.where(causal, new_scores, MASKED)
    final_top = jnp.maximum(merged_top, jnp.max(new_masked, axis=-1))
    rescale = jnp.exp(merged_top - final_top)
    new_weights = jnp.where(causal, jnp.exp(new_masked - final_top[..., None]), 0.0)
    final_total = merged_total * rescale + jnp.sum(new_weights, axis=-1)
    final_sum = merged_sum * rescale[..., None] + jnp.einsum(
        "bkgst,tbkd->bkgsd",
        new_weights.astype(jnp.bfloat16),
        value_part,
        preferred_element_type=jnp.float32,
    )
    attended = jnp.transpose(final_sum / final_total[..., None], (3, 0, 1, 2, 4))
    attended = attended.reshape(step_count, batch_count, query_width).astype(jnp.bfloat16)
    shard_cols = w_out.shape[1]
    projected = jnp.dot(
        attended.reshape(-1, query_width), w_out, preferred_element_type=jnp.float32
    )
    stream_shard = lax.dynamic_slice_in_dim(stream, rank * shard_cols, shard_cols, 2)
    mid_shard = stream_shard + projected.reshape(step_count, batch_count, shard_cols)
    mid_rows = lax.all_gather(mid_shard, SEQ, axis=2, tiled=True)
    normed_mid = rms_normalize(mid_rows, mlp_gain)
    flat_rows = normed_mid.reshape(-1, model_width)
    gate = jnp.dot(flat_rows, w_gate, preferred_element_type=jnp.float32)
    upper = jnp.dot(flat_rows, w_up, preferred_element_type=jnp.float32)
    hidden = (jax.nn.silu(gate) * upper).astype(jnp.bfloat16)
    down_terms = jnp.dot(hidden, w_down, preferred_element_type=jnp.float32).reshape(
        step_count, batch_count, model_width
    )
    summed = scatter_axes(down_terms, SEQ, (2, 1, 0), 2)
    layer_out = (mid_shard + summed).astype(jnp.bfloat16)
    return (attended, layer_out)


def solution(mesh):
    finer = Mesh(
        mesh.devices.reshape(mesh.shape["parts"], 8, 8, 2), ("parts", "seq_0", "seq_1", "seq_2")
    )
    return jax.shard_map(
        body,
        mesh=finer,
        in_specs=(
            P(None, "parts"),
            P("parts"),
            P(SEQ, None),
            P(),
            P(SEQ, None),
            P(),
            P("parts", SEQ, None),
            P("parts", SEQ, None),
            P(None, SEQ),
            P(),
            P(None, SEQ),
            P(None, SEQ),
            P(SEQ, None),
        ),
        out_specs=(P(None, "parts", None), P(None, "parts", SEQ)),
        check_vma=False,
    )
```

profile of v0, /device:TPU:528, one launch (start us, length us, event | category | flops | bytes accessed | tf_op | source)
XLA Modules:
  0.0 717.2 jit_solution(17745230185070453889)
XLA Ops:
  7.3 0.8 compare_and_fusion
  8.3 4.2 gather_fusion
  12.8 0.8 convert_select_fusion
  13.9 0.1 multiply_cosine_fusion
  14.0 0.3 copy.256
  14.4 1.1 copy-done.3
  15.5 0.3 copy.257
  15.8 1.1 bitcast_bitcast_fusion
  16.9 195.6 %all-reduce.14.cloned.1.call-done = f32[4,2,5120]{2,1,0:T(2,128)} async-done(((f32[4,2,5120]{2,1,0:T(2,128)}), f32[4,2,5120]{2,1,0:T(2,128)}) %all-reduce.14.cloned.1.call-update) | async-done | bytes 163856 | tf_op jit(solution)/shard_map/psum | solution.py:125
  212.4 1.1 multiply_reduce_fusion.1
  213.5 1.1 multiply_convert_fusion.1
  214.6 1.0 fusion.77
  215.8 181.4 %all-reduce.16.cloned.1.call-done = f32[8,7168]{1,0:T(8,128)} async-done(((f32[8,7168]{1,0:T(8,128)}), f32[8,7168]{1,0:T(8,128)}) %all-reduce.16.cloned.1.call-update) | async-done | bytes 229392 | tf_op jit(solution)/shard_map/psum | solution.py:130
  397.2 1.0 add_convert_fusion
  398.3 0.3 subtract_convert_fusion
  398.6 0.5 fusion.92
  399.2 0.2 copy.205
  399.4 0.3 fusion.13
  399.7 0.2 copy.206
  399.9 0.1 reshape.1056
  400.1 1.5 fusion.9
  401.6 0.7 maximum_bitcast_fusion
  402.4 38.6 %all-gather.9.cloned.1.call-done = f32[8,326,128]{2,1,0:T(8,128)} async-done(((f32[1,326,128]{2,1,0:T(8,128)}), f32[8,326,128]{2,1,0:T(8,128)}) %all-gather.9.cloned.1.call-update) | async-done | bytes 1335312 | tf_op jit(solution)/shard_map/all_gather | solution.py:25
  441.0 0.8 fusion.88
  442.1 2.0 fusion.39
  444.1 0.7 maximum_bitcast_fusion.1
  445.1 0.8 fusion.93
  445.9 0.1 copy.221
  446.0 38.5 %all-gather.11.cloned.1.call-done = f32[8,326,128]{2,1,0:T(8,128)} async-done(((f32[1,326,128]{2,1,0:T(8,128)}), f32[8,326,128]{2,1,0:T(8,128)}) %all-gather.11.cloned.1.call-update) | async-done | bytes 1335312 | tf_op jit(solution)/shard_map/all_gather | solution.py:25
  484.5 0.8 fusion.87
  485.6 2.0 fusion.18
  487.6 2.1 all-gather.5
  489.8 0.1 copy.212
  490.1 0.1 copy.213
  490.3 0.1 copy.223
  490.4 0.2 fusion.60
  490.6 0.1 copy.227
  490.8 0.1 copy.225
  491.1 0.1 copy.226
  491.3 0.1 copy.214
  491.4 0.1 copy.217
  491.5 0.1 copy.222
  491.7 0.1 copy.228
  491.8 0.5 fusion.4
  492.4 0.4 copy-done.10
  492.8 1.0 convolution_add_fusion.1
  493.9 56.9 %all_gather.27 = f32[4,2,5120]{0,1,2:T(2,128)} all-gather(f32[4,2,40]{0,1,2:T(2,128)S(1)} %copy.230), channel_id=1, replica_groups=mesh['parts'=2,'seq_0'=8,'seq_1'=8,'seq_2'=2] {'seq_0','seq_1','seq_2'}, dimensions={2}, use_global_device_ids=true | all-gather | bytes 165120 | tf_op jit(solution)/shard_map/all_gather | solution.py:191
  550.8 5.6 copy.233
  556.5 7.0 multiply_reduce_fusion
  564.0 0.3 fusion.94
  564.2 1.9 fusion.8
  566.1 0.4 reshape_reshape.2
  566.5 0.2 copy.235
  566.7 1.1 copy.236
  568.0 0.6 dynamic-slice
  569.3 30.1 %all-reduce.18.cloned.1.call-done = f32[128,4,2,40]{3,1,2,0:T(4,128)} async-done(((f32[128,4,2,40]{3,1,2,0:T(4,128)}), f32[128,4,2,40]{3,1,2,0:T(4,128)}) %all-reduce.18.cloned.1.call-update) | async-done | bytes 163856
  599.4 1.7 constant_dynamic-slice_fusion.2
  601.1 0.6 dynamic-slice.2
  601.7 0.6 dynamic-slice.4
  603.0 75.6 %all-reduce.20.cloned.1.call-done = f32[64,4,2,40]{3,1,2,0:T(4,128)} async-done(((f32[64,4,2,40]{3,1,2,0:T(4,128)}), f32[64,4,2,40]{3,1,2,0:T(4,128)}) %all-reduce.20.cloned.1.call-update) | async-done | bytes 81936
  678.7 0.8 constant_dynamic-slice_fusion.1
  679.4 29.7 %all-reduce.8 = f32[8,4,2,40]{3,1,2,0:T(4,128)S(1)} all-reduce(f32[8,4,2,40]{3,1,2,0:T(4,128)S(1)} %constant_dynamic-slice_fusion.1), channel_id=7, replica_groups=mesh['parts'=2,'seq_0'=8,'seq_1'=8,'seq_2'=2] {'seq_0'}, use_global_device_ids=true, to_apply=%region_10.11.clone | all-reduce | flops 2560 | bytes 20480
  709.1 0.6 constant_dynamic-slice_fusion
  709.7 0.6 fusion.70
  (105 shorter events, 3.4 us)
Async XLA Ops:
  7.2 557.1 %copy-start = (bf16[128,5120]{1,0:T(8,128)(2,1)S(1)}, bf16[128,5120]{1,0:T(8,128)(2,1)}, u32[]{:S(2)}) copy-start(bf16[128,5120]{1,0:T(8,128)(2,1)} %param.25) | copy-start | bytes 3932164
  7.2 6.6 copy-start.7
  7.2 6.6 copy-start.9
  7.2 6.8 copy-start.2
  7.2 205.2 %all-reduce.14.cloned.1.call-start = ((), (), s32[]{:S(2)}) async-start(), calls=%async_computation | async-start | bytes 327680 | tf_op jit(solution)/shard_map/psum | solution.py:125
  13.7 383.5 %all-reduce.16.cloned.1.call-start = ((), (), s32[]{:S(2)}) async-start(), calls=%async_computation.1 | async-start | bytes 458752 | tf_op jit(solution)/shard_map/psum | solution.py:130
  14.3 1.2 copy-start.3
  15.8 198.8 %copy-start.4 = (bf16[40,7168]{1,0:T(8,128)(2,1)S(1)}, bf16[40,7168]{1,0:T(8,128)(2,1)}, u32[]{:S(2)}) copy-start(bf16[40,7168]{1,0:T(8,128)(2,1)} %param.17) | copy-start | bytes 1720324
  16.9 380.3 %copy-start.6 = (f32[7168]{0:T(1024)S(1)}, f32[7168]{0:T(1024)}, u32[]{:S(2)}) copy-start(f32[7168]{0:T(1024)} %param.18) | copy-start | bytes 86020
  215.7 225.3 %all-gather.9.cloned.1.call-start = ((), (), s32[]{:S(2)}) async-start(), calls=%async_computation.2 | async-start | bytes 1511424 | tf_op jit(solution)/shard_map/all_gather | solution.py:25
  402.3 42.6 %copy-start.8 = (bf16[5120]{0:T(1024)(128)(2,1)S(1)}, bf16[5120]{0:T(1024)(128)(2,1)}, u32[]{:S(2)}) copy-start(bf16[5120]{0:T(1024)(128)(2,1)} %param.22) | copy-start | bytes 30724
  402.3 82.2 %all-gather.11.cloned.1.call-start = ((), (), s32[]{:S(2)}) async-start(), calls=%async_computation.3 | async-start | bytes 1511424 | tf_op jit(solution)/shard_map/all_gather | solution.py:25
  444.8 154.6 %all-reduce.18.cloned.1.call-start = ((), (), s32[]{:S(2)}) async-start(), calls=%async_computation.4 | async-start | bytes 1048576
  491.8 1.0 copy-start.10
  492.8 58.0 %copy-start.5 = (bf16[4,2,5120]{2,1,0:T(2,128)(2,1)}, bf16[4,2,5120]{2,1,0:T(2,128)(2,1)S(1)}, u32[]{:S(2)}) copy-start(bf16[4,2,5120]{2,1,0:T(2,128)(2,1)S(1)} %convert_element_type.84) | copy-start | bytes 245764
  556.5 7.5 %copy-start.1 = (bf16[5120,128]{1,0:T(8,128)(2,1)S(1)}, bf16[5120,128]{1,0:T(8,128)(2,1)}, u32[]{:S(2)}) copy-start(bf16[5120,128]{1,0:T(8,128)(2,1)} %param.23) | copy-start | bytes 3932164
  566.5 1.5 copy-start.13
  566.7 34.4 %copy-start.12 = (u32[256]{0:T(256)S(1)}, u32[256]{0:T(256)}, u32[]{:S(2)}) copy-start(u32[256]{0:T(256)} %constant.90) | copy-start | bytes 3076
  566.7 35.0 %copy-start.11 = (u32[256]{0:T(256)S(1)}, u32[256]{0:T(256)}, u32[]{:S(2)}) copy-start(u32[256]{0:T(256)} %constant.94) | copy-start | bytes 3076
  567.9 110.7 %all-reduce.20.cloned.1.call-start = ((), (), s32[]{:S(2)}) async-start(), calls=%async_computation.5 | async-start | bytes 524288
Sparse Core Ops, SparseCore 0:
  13.8 198.6 all-reduce.13
  215.8 181.3 all-reduce.15
  402.5 38.5 all-gather.8
  444.9 39.5 all-gather.10
  568.1 31.3 all-reduce.17
  601.6 77.0 all-reduce.19
where the time goes:
time: 718 us; the launch traced here: 717 us
  waiting for transfers between devices  560 us (78%)
  blocking collectives  88.7 us (12%)
  local copies, waits for them, and re-layouts  25.4 us (4%)
  other arithmetic  19.2 us (3%)
  between operations  16 us (2%)
  matrix products  7.37 us (1%)
    psum x1, waiting for transfers between devices, body(): stream = lax.psum(partial_rows, SEQ)  196 us
    psum x1, waiting for transfers between devices, body(): joint_summed = lax.psum(joint_partial, SEQ)  181 us
    unnamed x8, waiting for transfers between devices  106 us
    all_gather x2, waiting for transfers between devices, gathered_once(): both, at, found = (lax.all_gather(jnp.concatenate(lines), axis), 0, {})  77.1 us
    all_gather x1, blocking collectives, body(): mid_rows = lax.all_gather(mid_shard, SEQ, axis=2, tiled=True)  56.9 us
    unnamed x1, blocking collectives  29.7 us
  transfers between devices with their start and end apart: 6, of which 6 were waited for; matrix products, arithmetic and copies ran while one was open for 1% of the time, Pallas kernels for 0%

commit v1 on v0

--- a/solution.py
+++ b/solution.py
@@ -188,7 +188,8 @@
     )
     stream_shard = lax.dynamic_slice_in_dim(stream, rank * shard_cols, shard_cols, 2)
     mid_shard = stream_shard + projected.reshape(step_count, batch_count, shard_cols)
-    mid_rows = lax.all_gather(mid_shard, SEQ, axis=2, tiled=True)
+    repeated = jnp.stack([mid_shard] * lax.axis_size(SEQ))
+    mid_rows = jnp.concatenate(lax.all_to_all(repeated, SEQ, 0, 0), axis=2)
     normed_mid = rms_normalize(mid_rows, mlp_gain)
     flat_rows = normed_mid.reshape(-1, model_width)
     gate = jnp.dot(flat_rows, w_gate, preferred_element_type=jnp.float32)

time: 718 us -> 673 us (0.937)
  blocking collectives: 88.7 us -> 31.8 us
  starting transfers between devices: 0.38 us -> 13.3 us
    all_gather x1 -> x0, blocking collectives: 56.9 us -> none  [body(): mid_rows = lax.all_gather(mid_shard, SEQ, axis=2, tiled=True)]
    all_to_all x0 -> x1, starting transfers between devices: none -> 13 us  [body(): mid_rows = jnp.concatenate(lax.all_to_all(repeated, SEQ, 0, 0), axis=2)]
    all_to_all x0 -> x1, waiting for transfers between devices: none -> 12.1 us  [body(): mid_rows = jnp.concatenate(lax.all_to_all(repeated, SEQ, 0, 0), axis=2)]
  transfers between devices with their start and end apart: 6 -> 7, of which waited for: 6 -> 7; matrix products, arithmetic and copies ran while one was open for 1% -> 1% of each run, Pallas kernels for 0% -> 0%
where the time goes in v1:
time: 673 us; the launch traced here: 672 us
  waiting for transfers between devices  567 us (84%)
  blocking collectives  31.8 us (5%)
  local copies, waits for them, and re-layouts  22.6 us (3%)
  between operations  16.1 us (2%)
  other arithmetic  14.3 us (2%)
  starting transfers between devices  13.3 us (2%)
  matrix products  6.87 us (1%)
    psum x1, waiting for transfers between devices, body(): stream = lax.psum(partial_rows, SEQ)  196 us
    psum x1, waiting for transfers between devices, body(): joint_summed = lax.psum(joint_partial, SEQ)  181 us
    unnamed x8, waiting for transfers between devices  101 us
    all_gather x2, waiting for transfers between devices, gathered_once(): both, at, found = (lax.all_gather(jnp.concatenate(lines), axis), 0, {})  77.2 us
    unnamed x1, blocking collectives  29.7 us
  transfers between devices with their start and end apart: 7, of which 7 were waited for; matrix products, arithmetic and copies ran while one was open for 1% of the time, Pallas kernels for 0%

profile of v1, /device:TPU:528, one launch (start us, length us, event | category | flops | bytes accessed | tf_op | source)
XLA Modules:
  0.0 672.0 jit_solution(771254569476138488)
XLA Ops:
  7.3 0.8 compare_and_fusion
  8.3 4.2 gather_fusion
  12.6 0.8 convert_select_fusion
  13.8 0.3 copy.226
  14.1 1.1 copy-done.3
  15.3 0.3 copy.227
  15.5 1.0 bitcast_bitcast_fusion
  16.6 195.6 %all-reduce.14.cloned.1.call-done = f32[4,2,5120]{2,0,1:T(4,128)} async-done(((f32[4,2,5120]{2,0,1:T(4,128)}), f32[4,2,5120]{2,0,1:T(4,128)}) %all-reduce.14.cloned.1.call-update) | async-done | bytes 163856 | tf_op jit(solution)/shard_map/psum | solution.py:125
  212.2 1.0 multiply_reduce_fusion.1
  213.3 1.0 multiply_convert_fusion.1
  214.4 1.0 fusion.79
  215.6 181.4 %all-reduce.16.cloned.1.call-done = f32[8,7168]{1,0:T(8,128)} async-done(((f32[8,7168]{1,0:T(8,128)}), f32[8,7168]{1,0:T(8,128)}) %all-reduce.16.cloned.1.call-update) | async-done | bytes 229392 | tf_op jit(solution)/shard_map/psum | solution.py:130
  397.0 1.0 add_convert_fusion
  398.1 0.3 subtract_convert_fusion
  398.4 0.5 fusion.95
  398.9 0.2 copy.175
  399.2 0.3 fusion.13
  399.6 0.2 copy.176
  399.9 1.5 fusion.9
  401.4 0.7 maximum_bitcast_fusion
  402.2 38.6 %all-gather.9.cloned.1.call-done = f32[8,326,128]{2,1,0:T(8,128)} async-done(((f32[1,326,128]{2,1,0:T(8,128)}), f32[8,326,128]{2,1,0:T(8,128)}) %all-gather.9.cloned.1.call-update) | async-done | bytes 1335312 | tf_op jit(solution)/shard_map/all_gather | solution.py:25
  440.8 0.8 fusion.91
  441.8 2.0 fusion.40
  443.8 0.7 maximum_bitcast_fusion.1
  444.8 0.8 fusion.96
  445.7 38.6 %all-gather.11.cloned.1.call-done = f32[8,326,128]{2,1,0:T(8,128)} async-done(((f32[1,326,128]{2,1,0:T(8,128)}), f32[8,326,128]{2,1,0:T(8,128)}) %all-gather.11.cloned.1.call-update) | async-done | bytes 1335312 | tf_op jit(solution)/shard_map/all_gather | solution.py:25
  484.3 0.8 fusion.90
  485.3 2.0 fusion.19
  487.3 2.1 all-gather.5
  489.6 0.1 copy.182
  489.9 0.1 copy.195
  490.1 0.1 copy.183
  490.3 0.1 copy.193
  490.4 0.2 fusion.61
  490.8 0.1 copy.196
  491.0 0.1 copy.198
  491.5 0.5 fusion.4
  492.2 0.4 copy-done.10
  492.5 0.3 fusion.14
  492.8 0.8 copy_add_fusion
  493.6 0.1 stack.2
  493.8 1.6 reshape.1156
  495.3 13.0 %all-to-all-start = ((f32[128,1,320]{2,1,0:T(1,128)}), f32[128,1,320]{2,1,0:T(1,128)S(1)}, u32[]{:S(2)}, u32[]{:S(2)}) async-start(f32[128,1,320]{2,1,0:T(1,128)} %reshape.1156), calls=%async_computation | async-start | bytes 393216 | tf_op jit(solution)/shard_map/all_to_all | solution.py:192
  508.4 12.1 %all-to-all-done = f32[128,1,320]{2,1,0:T(1,128)S(1)} async-done(((f32[128,1,320]{2,1,0:T(1,128)}), f32[128,1,320]{2,1,0:T(1,128)S(1)}, u32[]{:S(2)}, u32[]{:S(2)}) %all-to-all-start) | async-done | bytes 163872 | tf_op jit(solution)/shard_map/all_to_all | solution.py:192
  520.5 0.5 broadcast.229
  521.0 1.1 reduce.73
  522.1 0.8 reshape.1157
  522.9 0.4 multiply_reduce_fusion
  523.5 0.3 reshape.1085
  523.8 1.7 fusion.86
  525.6 0.6 fusion.8
  526.2 0.4 reshape_reshape.2
  526.6 0.2 copy.205
  526.8 1.1 copy.206
  528.1 0.6 dynamic-slice
  529.3 24.9 %all-reduce.18.cloned.1.call-done = f32[128,4,2,40]{3,1,2,0:T(4,128)} async-done(((f32[128,4,2,40]{3,1,2,0:T(4,128)}), f32[128,4,2,40]{3,1,2,0:T(4,128)}) %all-reduce.18.cloned.1.call-update) | async-done | bytes 163856
  554.3 1.7 constant_dynamic-slice_fusion.1
  556.0 0.7 dynamic-slice.4
  556.7 0.6 dynamic-slice.2
  557.9 75.6 %all-reduce.20.cloned.1.call-done = f32[64,4,2,40]{3,1,2,0:T(4,128)} async-done(((f32[64,4,2,40]{3,1,2,0:T(4,128)}), f32[64,4,2,40]{3,1,2,0:T(4,128)}) %all-reduce.20.cloned.1.call-update) | async-done | bytes 81936
  633.5 0.8 constant_dynamic-slice_fusion
  634.2 29.7 %all-reduce.8 = f32[8,4,2,40]{3,1,2,0:T(4,128)S(1)} all-reduce(f32[8,4,2,40]{3,1,2,0:T(4,128)S(1)} %constant_dynamic-slice_fusion), channel_id=7, replica_groups=mesh['parts'=2,'seq_0'=8,'seq_1'=8,'seq_2'=2] {'seq_0'}, use_global_device_ids=true, to_apply=%region_10.11.clone | all-reduce | flops 2560 | bytes 20480
  663.9 0.7 fusion.72
  664.6 0.6 copy.207
  (108 shorter events, 3.8 us)
Async XLA Ops:
  7.2 518.4 %copy-start = (bf16[128,5120]{1,0:T(8,128)(2,1)S(1)}, bf16[128,5120]{1,0:T(8,128)(2,1)}, u32[]{:S(2)}) copy-start(bf16[128,5120]{1,0:T(8,128)(2,1)} %param.25) | copy-start | bytes 3932164
  7.2 6.3 copy-start.9
  7.2 6.5 copy-start.7
  7.2 6.5 copy-start.2
  7.2 205.0 %all-reduce.14.cloned.1.call-start = ((), (), s32[]{:S(2)}) async-start(), calls=%async_computation.1 | async-start | bytes 327680 | tf_op jit(solution)/shard_map/psum | solution.py:125
  13.4 383.6 %all-reduce.16.cloned.1.call-start = ((), (), s32[]{:S(2)}) async-start(), calls=%async_computation.2 | async-start | bytes 458752 | tf_op jit(solution)/shard_map/psum | solution.py:130
  14.0 1.2 copy-start.3
  15.5 198.9 %copy-start.4 = (bf16[40,7168]{1,0:T(8,128)(2,1)S(1)}, bf16[40,7168]{1,0:T(8,128)(2,1)}, u32[]{:S(2)}) copy-start(bf16[40,7168]{1,0:T(8,128)(2,1)} %param.17) | copy-start | bytes 1720324
  16.6 380.4 %copy-start.6 = (f32[7168]{0:T(1024)S(1)}, f32[7168]{0:T(1024)}, u32[]{:S(2)}) copy-start(f32[7168]{0:T(1024)} %param.18) | copy-start | bytes 86020
  215.4 225.3 %all-gather.9.cloned.1.call-start = ((), (), s32[]{:S(2)}) async-start(), calls=%async_computation.3 | async-start | bytes 1511424 | tf_op jit(solution)/shard_map/all_gather | solution.py:25
  402.1 82.1 %all-gather.11.cloned.1.call-start = ((), (), s32[]{:S(2)}) async-start(), calls=%async_computation.4 | async-start | bytes 1511424 | tf_op jit(solution)/shard_map/all_gather | solution.py:25
  491.5 1.0 copy-start.10
  492.1 16.3 %copy-start.8 = (bf16[5120]{0:T(1024)(128)(2,1)S(1)}, bf16[5120]{0:T(1024)(128)(2,1)}, u32[]{:S(2)}) copy-start(bf16[5120]{0:T(1024)(128)(2,1)} %param.22) | copy-start | bytes 30724
  492.5 29.5 %copy-start.5 = (bf16[4,2,5120]{2,1,0:T(2,128)(2,1)}, bf16[4,2,5120]{2,1,0:T(2,128)(2,1)S(1)}, u32[]{:S(2)}) copy-start(bf16[4,2,5120]{2,1,0:T(2,128)(2,1)S(1)} %convert_element_type.85) | copy-start | bytes 245764
  495.3 25.1 %all-to-all-start = ((f32[128,1,320]{2,1,0:T(1,128)}), f32[128,1,320]{2,1,0:T(1,128)S(1)}, u32[]{:S(2)}, u32[]{:S(2)}) async-start(f32[128,1,320]{2,1,0:T(1,128)} %reshape.1156), calls=%async_computation | async-start | bytes 393216 | tf_op jit(solution)/shard_map/all_to_all | solution.py:192
  508.3 46.0 %all-reduce.18.cloned.1.call-start = ((), (), s32[]{:S(2)}) async-start(), calls=%async_computation.5 | async-start | bytes 1048576
  523.8 1.8 copy-start.1
  526.6 1.5 copy-start.13
  526.8 29.2 %copy-start.12 = (u32[256]{0:T(256)S(1)}, u32[256]{0:T(256)}, u32[]{:S(2)}) copy-start(u32[256]{0:T(256)} %constant.94) | copy-start | bytes 3076
  526.8 29.8 %copy-start.11 = (u32[256]{0:T(256)S(1)}, u32[256]{0:T(256)}, u32[]{:S(2)}) copy-start(u32[256]{0:T(256)} %constant.90) | copy-start | bytes 3076
  528.0 105.4 %all-reduce.20.cloned.1.call-start = ((), (), s32[]{:S(2)}) async-start(), calls=%async_computation.6 | async-start | bytes 524288
Sparse Core Ops, SparseCore 0:
  13.5 198.6 all-reduce.13
  215.6 181.3 all-reduce.15
  402.2 38.5 all-gather.8
  444.7 39.5 all-gather.10
  528.1 26.0 all-reduce.17
  556.4 76.9 all-reduce.19
